TPU v7x, 32 devices: a whole 2x2x4 slice. The times are simulated.
32 devices in a mesh: rep: 2 (over x), tp: 4 (over z), sp: 4 (over y, core).
Axes of the slice: x: 2, y: 2, z: 4, core: 2. Of those that a mesh axis runs over, the one named last changes fastest.
Arguments:
- x: bfloat16 [8192, 5376], P(('rep', 'sp')), parts along dimension 0
- pos: int32 [8192], P(('rep', 'sp')), parts along dimension 0
- g1: float32 [5376], replicated
- g2: float32 [5376], replicated
- wq: bfloat16 [5376, 4096], P(None, 'tp')
- wk: bfloat16 [5376, 2048], P(None, 'tp')
- wv: bfloat16 [5376, 2048], P(None, 'tp')
- wo: bfloat16 [4096, 5376], P('tp')
- w1: bfloat16 [5376, 21504], P(None, 'tp')
- w3: bfloat16 [5376, 21504], P(None, 'tp')
- w2: bfloat16 [21504, 5376], P('tp')
Outputs:
- output 1: bfloat16 [8192, 5376], P(('rep', 'sp')), parts along dimension 0
- output 2: bfloat16 [8192, 16, 128], P('rep', ('tp', 'sp')), parts along dimension 0
- output 3: bfloat16 [8192, 16, 128], P('rep', ('tp', 'sp')), parts along dimension 0
There are 2 independent parts. A program takes and returns all parts, laid end to end along the dimension named above; an argument that names none is the same for every part.
All inputs are finite; a program needn't handle non-finite values.
Results may differ from a plain program's by a relative error of at most 0.00743013.
Values are sent between devices in bfloat16 or wider.
A program may use at most 1 GiB of HBM per device.

v0:
```python
import functools

import jax
import jax.numpy as jnp
from jax import lax
from jax.experimental import pallas as pl
from jax.experimental.pallas import tpu as pltpu
from jax.sharding import PartitionSpec as P


HEAD_DIM = 128
EPS = 1e-5
ROPE_BASE = 5e5
NEG = -1e30
QB = 512
KB = 512
TILE = 256
LAG = 2
RING = 3 * LAG + 2
MROWS = 256
MESH = pl.DeviceIdType.MESH


def _rms(x, g):
    x32 = x.astype(jnp.float32)
    r = lax.rsqrt(jnp.mean(x32 * x32, axis=-1, keepdims=True) + EPS)
    return (x32 * r * g).astype(jnp.bfloat16)


def _angles(pos):
    half = HEAD_DIM // 2
    inv = ROPE_BASE ** (-2.0 * jnp.arange(half, dtype=jnp.float32) / HEAD_DIM)
    ang = pos.astype(jnp.float32)[..., None] * inv
    return jnp.cos(ang)[..., None, :], jnp.sin(ang)[..., None, :]


def _rope(t, cs):
    c, s = cs
    half = HEAD_DIM // 2
    t1, t2 = t[..., :half], t[..., half:]
    return jnp.concatenate([t1 * c - t2 * s, t2 * c + t1 * s], axis=-1)


def _attn_kernel(q_ref, k_ref, v_ref, o_ref, *, heads, per_src):
    i = pl.program_id(0)
    scale = HEAD_DIM ** -0.5
    q = q_ref[0].reshape(heads * QB, HEAD_DIM)
    rows = heads * QB

    def scores(j):
        kb = k_ref[j // per_src, 0, pl.ds((j % per_src) * KB, KB), :]
        return lax.dot_general(q, kb, (((1,), (1,)), ((), ())), preferred_element_type=jnp.float32) * scale

    def update(j, s, carry):
        m, l, acc = carry
        mn = jnp.maximum(m, jnp.max(s, axis=1, keepdims=True))
        a = jnp.exp(m - mn)
        p = jnp.exp(s - mn)
        l = l * a + jnp.sum(p, axis=1, keepdims=True)
        vb = v_ref[j // per_src, 0, pl.ds((j % per_src) * KB, KB), :]
        acc = acc * a + jnp.dot(p.astype(jnp.bfloat16), vb, preferred_element_type=jnp.float32)
        return mn, l, acc

    init = (
        jnp.full((rows, 1), NEG, jnp.float32),
        jnp.zeros((rows, 1), jnp.float32),
        jnp.zeros((rows, HEAD_DIM), jnp.float32),
    )
    carry = lax.fori_loop(0, i, lambda j, c: update(j, scores(j), c), init)
    r = lax.broadcasted_iota(jnp.int32, (heads, QB, KB), 1)
    c = lax.broadcasted_iota(jnp.int32, (heads, QB, KB), 2)
    s = jnp.where((r >= c).reshape(rows, KB), scores(i), NEG)
    _, l, acc = update(i, s, carry)
    o = (acc / l).astype(jnp.bfloat16)
    for h in range(heads):
        o_ref[0, :, h * HEAD_DIM:(h + 1) * HEAD_DIM] = o[h * QB:(h + 1) * QB]


def _attention(buf, heads):
    sp, _, m, dh = buf.shape
    per = m // QB
    n = sp * m
    return pl.pallas_call(
        functools.partial(_attn_kernel, heads=heads, per_src=m // KB),
        grid=(n // QB,),
        in_specs=[
            pl.BlockSpec((1, heads, QB, dh), lambda i: (i // per, 0, i % per, 0)),
            pl.BlockSpec((sp, 1, m, dh), lambda i: (0, heads, 0, 0)),
            pl.BlockSpec((sp, 1, m, dh), lambda i: (0, heads + 1, 0, 0)),
        ],
        out_specs=pl.BlockSpec((1, QB, heads * dh), lambda i: (i // per, i % per, 0)),
        out_shape=jax.ShapeDtypeStruct((sp, m, heads * dh), jnp.bfloat16),
        cost_estimate=pl.CostEstimate(flops=4 * heads * n * n * dh, bytes_accessed=8 * n * dh * 2, transcendentals=heads * n * n // 2),
        compiler_params=pltpu.CompilerParams(vmem_limit_bytes=48 * 1024 * 1024),
        name="attn",
    )(buf, buf, buf)


def _hop(up, dn, k):
    up = lax.ppermute(up, "tp", [(i, i + 1) for i in range(k - 1, 3)])
    dn = lax.ppermute(dn, "tp", [(i, i - 1) for i in range(1, 5 - k)])
    return up, dn


def _side_by_side(a, up, dn, t):
    out = []
    for s in range(4):
        b = a
        for d in range(4):
            if d < s:
                b = jnp.where(t == d, dn[s - d - 1], b)
            elif d > s:
                b = jnp.where(t == d, up[d - s - 1], b)
        out.append(b)
    return jnp.concatenate(out, axis=1)


def _mlp_kernel(hid_ref, u_ref, w1_ref, w3_ref, w2_ref, x0_ref, x1_ref, y_ref, acc, part, fin, hid, sf, rf, sb, rb, sl, *, nc, nt):
    i = pl.program_id(0)
    t = lax.axis_index("tp")
    m = part.shape[1]
    h = m // 2

    @pl.when(i == 0)
    def _():
        barrier = pltpu.get_barrier_semaphore()

        @pl.when(t > 0)
        def _():
            pl.semaphore_signal(barrier, inc=1, device_id={"tp": t - 1}, device_id_type=MESH)

        @pl.when(t < 3)
        def _():
            pl.semaphore_signal(barrier, inc=1, device_id={"tp": t + 1}, device_id_type=MESH)

        pl.semaphore_wait(barrier, jnp.where((t == 0) | (t == 3), 1, 2))

    def place(s, g):
        row = pl.multiple_of((g // nc) * m + s * h, h)
        return y_ref.at[pl.ds(row, h), pl.ds(pl.multiple_of((g % nc) * TILE, TILE), TILE)]

    def forward(s, g, dev):
        return pltpu.make_async_remote_copy(
            src_ref=acc.at[s, g], dst_ref=acc.at[s, g], send_sem=sf.at[s, g], recv_sem=rf.at[s, g],
            device_id={"tp": dev}, device_id_type=MESH)

    def back(s, g, dev, src):
        return pltpu.make_async_remote_copy(
            src_ref=src, dst_ref=place(s, g), send_sem=sb.at[s, g], recv_sem=rb.at[s, g],
            device_id={"tp": dev}, device_id_type=MESH)

    def keep(s, g):
        return pltpu.make_async_copy(fin.at[g % RING], place(s, g), sl.at[g])

    def settle(s, g, dev):
        back(s, g, dev, fin.at[g % RING]).wait_send()
        keep(s, g).wait()

    other = jnp.where(t < 2, t + 1, t - 1)
    for s in range(2):
        pos = 3 - t if s == 0 else t
        nxt = t - 1 if s == 0 else t + 1
        prv = t + 1 if s == 0 else t - 1
        rows = slice(s * h, (s + 1) * h)
        g = i - 1 - pos * LAG
        on = (g >= 0) & (g < nt)

        @pl.when(on & (pos == 0))
        def _():
            acc[s, g] = part[g % RING, rows, :]
            forward(s, g, nxt).start()

        @pl.when(on & (pos > 0) & (pos < 3))
        def _():
            forward(s, g, other).wait_recv()
            acc[s, g] = acc[s, g] + part[g % RING, rows, :]
            forward(s, g, nxt).start()

        @pl.when(on & (pos == 3))
        def _():
            forward(s, g, other).wait_recv()
            total = acc[s, g] + part[g % RING, rows, :]

            @pl.when(g >= RING)
            def _():
                settle(s, g - RING, prv)

            res = jnp.where(g < nc, x0_ref[rows, :].astype(jnp.float32), x1_ref[rows, :].astype(jnp.float32))
            fin[g % RING] = (res + total).astype(jnp.bfloat16)
            back(s, g, prv, fin.at[g % RING]).start()
            keep(s, g).start()

        gb = i - 1 - 3 * LAG - (3 - pos) * LAG
        onb = (gb >= 0) & (gb < nt)

        @pl.when(onb & (pos > 0) & (pos < 3))
        def _():
            back(s, gb, other, place(s, gb)).wait_recv()
            back(s, gb, prv, place(s, gb)).start()

        @pl.when(onb & (pos == 0))
        def _():
            back(s, gb, other, place(s, gb)).wait_recv()

    def blocks(body):
        def step(b, _):
            body(pl.ds(pl.multiple_of(b * MROWS, MROWS), MROWS))
            return 0

        lax.fori_loop(0, m // MROWS, step, 0)

    @pl.when(i < nc)
    def _():
        cols = pl.ds(pl.multiple_of(i * TILE, TILE), TILE)

        def body(r):
            a = jnp.dot(u_ref[r, :], w1_ref[...], preferred_element_type=jnp.float32)
            b = jnp.dot(u_ref[r, :], w3_ref[...], preferred_element_type=jnp.float32)
            hid[r, cols] = (jax.nn.silu(a) * b).astype(jnp.bfloat16)
            part[i % RING, r, :] = jnp.dot(hid_ref[r, :], w2_ref[...], preferred_element_type=jnp.float32)

        blocks(body)

    @pl.when((i >= nc) & (i < nt))
    def _():
        def body(r):
            part[i % RING, r, :] = jnp.dot(hid[r, :], w2_ref[...], preferred_element_type=jnp.float32)

        blocks(body)

    @pl.when(i == nt + 6 * LAG)
    def _():
        for s in range(2):
            pos = 3 - t if s == 0 else t

            def drain(g, _):
                @pl.when(pos < 3)
                def _():
                    forward(s, g, other).wait_send()

                @pl.when((pos > 0) & (pos < 3))
                def _():
                    back(s, g, other, place(s, g)).wait_send()

                @pl.when((pos == 3) & (g >= nt - RING))
                def _():
                    settle(s, g, other)

                return 0

            lax.fori_loop(0, nt, drain, 0)


def _mlp_out(hid, u, w1, w3, w2, xs):
    m, f = hid.shape
    d = w2.shape[1]
    nc = d // TILE
    nt = 2 * nc
    assert f == d

    def late(i):
        return jnp.clip(i - 1 - 3 * LAG, 0, nt - 1)

    once = pl.Buffered(1)
    return pl.pallas_call(
        functools.partial(_mlp_kernel, nc=nc, nt=nt),
        grid=(nt + 6 * LAG + 1,),
        in_specs=[
            pl.BlockSpec((m, f), lambda i: (0, 0), pipeline_mode=once),
            pl.BlockSpec((m, u.shape[1]), lambda i: (0, 0), pipeline_mode=once),
            pl.BlockSpec((w1.shape[0], TILE), lambda i: (0, jnp.minimum(i, nc - 1))),
            pl.BlockSpec((w3.shape[0], TILE), lambda i: (0, jnp.minimum(i, nc - 1))),
            pl.BlockSpec((f, TILE), lambda i: (0, jnp.where(i < nc, i, jnp.minimum(i - nc, nc - 1)))),
            pl.BlockSpec((m, TILE), lambda i: (0, jnp.minimum(late(i), nc - 1))),
            pl.BlockSpec((m, TILE), lambda i: (0, jnp.maximum(late(i) - nc, 0))),
        ],
        out_specs=pl.BlockSpec(memory_space=pl.ANY),
        out_shape=jax.ShapeDtypeStruct((2 * m, d), jnp.bfloat16),
        scratch_shapes=[
            pltpu.VMEM((2, nt, m // 2, TILE), jnp.float32),
            pltpu.VMEM((RING, m, TILE), jnp.float32),
            pltpu.VMEM((RING, m // 2, TILE), jnp.bfloat16),
            pltpu.VMEM((m, f), jnp.bfloat16),
            pltpu.SemaphoreType.DMA((2, nt)),
            pltpu.SemaphoreType.DMA((2, nt)),
            pltpu.SemaphoreType.DMA((2, nt)),
            pltpu.SemaphoreType.DMA((2, nt)),
            pltpu.SemaphoreType.DMA((nt,)),
        ],
        cost_estimate=pl.CostEstimate(flops=8 * m * f * d, bytes_accessed=6 * f * d + 12 * m * d, transcendentals=m * f),
        compiler_params=pltpu.CompilerParams(
            collective_id=0, has_side_effects=True, vmem_limit_bytes=67043328, dimension_semantics=("arbitrary",)),
        name="mlp_out",
    )(hid, u, w1, w3, w2, *xs)


def solution(mesh):
    sp = mesh.shape["sp"]
    nrep = mesh.shape["rep"]
    tok = P(("rep", "sp"), None)
    col = P(None, "tp")
    row = P("tp", None)
    cache = P("rep", ("tp", "sp"), None)

    def local(x, pos, g1, g2, wq, wk, wv, wo, w1, w3, w2):
        m, _ = x.shape
        n = m * sp
        ht = wq.shape[1] // HEAD_DIM
        kt = wk.shape[1] // HEAD_DIM
        qh = ht // sp
        t = lax.axis_index("tp")
        part = wo.shape[0] // (nrep * sp)
        mine = lax.axis_index("rep") * sp + lax.axis_index("sp")
        wo_all = lax.all_gather(lax.dynamic_slice_in_dim(wo, mine * part, part, 0), ("tp", "rep", "sp"), axis=0, tiled=True)

        u = _rms(x, g1)
        cs = _angles(pos)
        q = _rope(jnp.dot(u, wq, preferred_element_type=jnp.float32).reshape(m, ht, HEAD_DIM), cs).astype(jnp.bfloat16)
        k = _rope(jnp.dot(u, wk, preferred_element_type=jnp.float32).reshape(m, kt, HEAD_DIM), cs).astype(jnp.bfloat16)
        v = jnp.dot(u, wv, preferred_element_type=jnp.float32).astype(jnp.bfloat16).reshape(m, kt, HEAD_DIM)
        buf = jnp.concatenate([q.reshape(m, sp, qh, HEAD_DIM), k.reshape(m, sp, 1, HEAD_DIM), v.reshape(m, sp, 1, HEAD_DIM)], axis=2)
        buf = lax.all_to_all(buf.transpose(1, 2, 0, 3), "sp", 0, 0, tiled=True)
        ka = buf[:, qh].reshape(n, 1, HEAD_DIM)
        va = buf[:, qh + 1].reshape(n, 1, HEAD_DIM)
        att = _attention(buf, qh)
        att = lax.all_to_all(att, "sp", 0, 0, tiled=True)
        att = att.transpose(1, 0, 2).reshape(m, ht * HEAD_DIM)
        mc = m // 2
        a0, a1 = att[:mc], att[mc:]
        hops = [(a0, a0)]
        for k in range(1, 4):
            hops.append(_hop(*hops[-1], k))
        first = _side_by_side(a0, *zip(*hops[1:]), t)
        first, a1 = lax.optimization_barrier((first, a1))

        def mix(a, xr, g):
            o = jnp.dot(a, wo_all, preferred_element_type=jnp.float32)
            x1 = (xr.astype(jnp.float32) + o).astype(jnp.bfloat16)
            return x1, _rms(x1, g)

        hop1 = _hop(a1, a1, 1)
        x0, u0 = mix(first, x[:mc], g2)
        u0, hop1 = lax.optimization_barrier((u0, hop1))
        hop2 = _hop(*hop1, 2)
        h1 = jnp.dot(u0, w1, preferred_element_type=jnp.float32)
        u0, h1, hop2 = lax.optimization_barrier((u0, h1, hop2))
        hop3 = _hop(*hop2, 3)
        h3 = jnp.dot(u0, w3, preferred_element_type=jnp.float32)
        hid = (jax.nn.silu(h1) * h3).astype(jnp.bfloat16)
        hid, hop3, gb = lax.optimization_barrier((hid, hop3, g2))
        second = _side_by_side(a1, *zip(hop1, hop2, hop3), t)
        x1, u1 = mix(second, x[mc:], gb)
        y = _mlp_out(hid, u1, w1, w3, w2, (x0, x1))
        return y, ka, va

    return jax.shard_map(
        local,
        mesh=mesh,
        in_specs=(tok, P(("rep", "sp")), P(), P(), col, col, col, row, col, col, row),
        out_specs=(tok, cache, cache),
        check_vma=False,
    )
```

profile of v0, /device:TPU:0, one launch (start us, length us, event | category | flops | bytes accessed | tf_op | source)
XLA Modules:
  0.0 950.4 jit_solution(3540050986658749862)
XLA Ops:
  7.2 0.0 all-gather.2.cloned.1.call-start
  7.2 2.5 constant_dynamic-slice_fusion
  9.8 0.0 all-gather.2.cloned.1.call-update
  9.8 0.0 copy-start.2
  9.8 0.8 convert_element_type.52
  10.7 6.5 fusion
  17.1 9.8 %convolution_convert_fusion = bf16[1024,512]{0,1:T(8,128)(2,1)} fusion(bf16[5376,512]{1,0:T(8,128)(2,1)} %param.17, bf16[1024,5376]{1,0:T(8,128)(2,1)S(1)} %copy-done.2, f32[5376]{0:T(1024)S(1)} %copy-done.11, f32[1024]{0:T(1024)S(1)} %add_rsqrt_fusion), kind=kOutput, calls=%fused_computation.31 | convolution fusion | flops 5659688960 | bytes 17589248 | tf_op jit(solution)/shard_map/dot_general | solution.py:320
  26.9 2.4 copy.22
  29.4 10.8 %fusion.20 = f32[1024,512]{0,1:T(8,128)S(1)} fusion(bf16[5376,512]{1,0:T(8,128)(2,1)} %param.16, bf16[1024,5376]{1,0:T(8,128)(2,1)} %param.11, f32[5376]{0:T(1024)S(1)} %copy-done.11, f32[1024]{0:T(1024)S(1)} %add_rsqrt_fusion), kind=kOutput, calls=%fused_computation.50 | convolution fusion | flops 5659164672 | bytes 18637824 | tf_op jit(solution)/shard_map/dot_general | solution.py:319
  40.2 1.2 fusion.27
  41.3 1.8 copy.28
  43.2 1.9 copy.27
  45.1 19.4 %fusion.22 = f32[1024,1024]{0,1:T(8,128)} fusion(bf16[5376,1024]{1,0:T(8,128)(2,1)} %param.15, bf16[1024,5376]{1,0:T(8,128)(2,1)} %param.11, f32[5376]{0:T(1024)S(1)} %copy-done.11, f32[1024]{0:T(1024)S(1)} %add_rsqrt_fusion), kind=kOutput, calls=%fused_computation.51 | convolution fusion | flops 11296309248 | bytes 26240000 | tf_op jit(solution)/shard_map/dot_general | solution.py:318
  64.5 4.8 fusion.25
  69.3 3.9 copy.26
  73.2 4.3 copy.25
  77.4 0.0 copy-start
  77.5 1.9 multiply_cosine_fusion
  79.4 2.7 fusion.16
  82.1 0.0 copy-start.6
  82.1 1.2 subtract_convert_fusion
  83.3 0.0 copy-done.6
  83.3 2.4 maximum_bitcast_fusion
  85.7 58.8 %all_to_all.10.q_ref.k_ref.v_ref = bf16[4,4,1024,128]{3,2,1,0:T(8,128)(2,1)} all-to-all(bf16[4,4,1024,128]{3,2,1,0:T(8,128)(2,1)S(1)} %maximum_bitcast_fusion), channel_id=1, replica_groups=mesh['rep'=2,'tp'=4,'sp'=4] {'sp'}, dimensions={0} | all-to-all | bytes 8388608 | tf_op jit(solution)/shard_map/all_to_all | solution.py:322
  144.6 47.9 %attn.1 = bf16[4,1024,256]{2,1,0:T(8,128)(2,1)S(1)} custom-call(bf16[4,4,1024,128]{3,2,1,0:T(8,128)(2,1)} %all_to_all.10.q_ref.k_ref.v_ref, bf16[4,4,1024,128]{3,2,1,0:T(8,128)(2,1)} %all_to_all.10.q_ref.k_ref.v_ref, bf16[4,4,1024,128]{3,2,1,0:T(8,128)(2,1)} %all_to_all.10.q_ref.k_ref.v_ref), custom_call_target="tpu_custom_call" | custom-call | flops 17179869184 | bytes 8388608 | tf_op jit(solution)/shard_map/attn/pallas_call | solution.py:83
  192.4 46.6 %all_to_all.11 = bf16[4,1024,256]{2,1,0:T(8,128)(2,1)S(1)} all-to-all(bf16[4,1024,256]{2,1,0:T(8,128)(2,1)S(1)} %attn.1), channel_id=1, replica_groups=mesh['rep'=2,'tp'=4,'sp'=4] {'sp'}, dimensions={0} | all-to-all | bytes 4194304 | tf_op jit(solution)/shard_map/all_to_all | solution.py:326
  239.0 0.1 fusion.26
  239.2 0.5 copy.23
  239.7 1.3 collective-permute-start.3
  241.0 4.9 collective-permute-start
  245.9 53.6 %collective-permute-done.3 = bf16[512,1024]{0,1:T(8,128)(2,1)S(1)} collective-permute-done((bf16[512,1024]{0,1:T(8,128)(2,1)S(1)}, bf16[512,1024]{0,1:T(8,128)(2,1)S(1)}, u32[]{:S(2)}, u32[]{:S(2)}) %collective-permute-start.3) | collective-permute-done | bytes 1048608 | tf_op jit(solution)/shard_map/ppermute | solution.py:101
  299.5 1.3 collective-permute-start.4
  300.8 0.0 collective-permute-done
  300.8 0.0 copy-start.8
  300.8 1.7 collective-permute-start.1
  302.5 24.1 %collective-permute-done.4 = bf16[512,1024]{0,1:T(8,128)(2,1)} collective-permute-done((bf16[512,1024]{0,1:T(8,128)(2,1)S(1)}, bf16[512,1024]{0,1:T(8,128)(2,1)}, u32[]{:S(2)}, u32[]{:S(2)}) %collective-permute-start.4) | collective-permute-done | bytes 1048608 | tf_op jit(solution)/shard_map/ppermute | solution.py:101
  326.6 1.3 collective-permute-start.5
  327.9 0.0 collective-permute-done.1
  327.9 1.7 collective-permute-start.2
  329.6 3.0 fusion.24
  332.6 0.5 copy.24
  333.2 20.0 %collective-permute-done.5 = bf16[512,1024]{0,1:T(8,128)(2,1)} collective-permute-done((bf16[512,1024]{0,1:T(8,128)(2,1)}, bf16[512,1024]{0,1:T(8,128)(2,1)}, u32[]{:S(2)}, u32[]{:S(2)}) %collective-permute-start.5) | collective-permute-done | bytes 1048608 | tf_op jit(solution)/shard_map/ppermute | solution.py:101
  353.1 0.0 collective-permute-done.2
  353.1 3.0 select_select_fusion.7
  356.1 2.2 pad_maximum_fusion
  358.2 1.4 collective-permute-start.7
  359.7 5.5 collective-permute-start.6
  365.2 31.8 %fusion.3 = (f32[512]{0:T(512)S(1)}, bf16[512,5376]{1,0:T(8,128)(2,1)S(1)}) fusion(bf16[512,4096]{0,1:T(8,128)(2,1)} %pad_maximum_fusion, bf16[4096,5376]{1,0:T(8,128)(2,1)} %all-gather.2.cloned.1.call-done, bf16[1024,5376]{1,0:T(8,128)(2,1)} %param.11), kind=kOutput, calls=%fused_computation.9 | convolution fusion | flops 22565093376 | bytes 59246592 | tf_op jit(solution)/shard_map/dot_general | solution.py:337
  397.0 2.3 copy-done.3
  399.3 4.3 fusion.5
  403.7 0.0 collective-permute-done.7
  403.7 0.0 collective-permute-done.6
  403.7 0.7 collective-permute-start.8
  404.4 1.3 collective-permute-start.9
  405.7 40.6 %fusion.28 = f32[512,5376]{1,0:T(8,128)} fusion(bf16[512,5376]{1,0:T(8,128)(2,1)} %fusion.5, bf16[5376,5376]{1,0:T(8,128)(2,1)} %w1_ref.1), kind=kOutput, calls=%fused_computation.56 | convolution fusion | flops 29595009024 | bytes 74317824 | tf_op jit(solution)/shard_map/dot_general | solution.py:345
  446.3 0.0 collective-permute-done.8
  446.4 0.9 collective-permute-start.10
  447.2 1.3 collective-permute-start.11
  448.5 42.8 %multiply_convert_fusion.hid_ref = bf16[512,5376]{1,0:T(8,128)(2,1)} fusion(f32[512,5376]{1,0:T(8,128)} %fusion.28, bf16[512,5376]{1,0:T(8,128)(2,1)} %fusion.5, bf16[5376,5376]{1,0:T(8,128)(2,1)} %w3_ref.1), kind=kOutput, calls=%fused_computation.16 | convolution fusion | flops 29611524096 | bytes 79822848 | tf_op jit(solution)/shard_map/dot_general | solution.py:348
  491.3 3.0 select_select_fusion.3
  494.3 32.9 %fusion.6 = (f32[512]{0:T(512)S(1)}, bf16[512,5376]{1,0:T(8,128)(2,1)}) fusion(bf16[4096,5376]{1,0:T(8,128)(2,1)} %all-gather.2.cloned.1.call-done, bf16[512,1024]{0,1:T(8,128)(2,1)} %get-tuple-element.40, bf16[512,1024]{0,1:T(8,128)(2,1)} %get-tuple-element.39, bf16[512,1024]{0,1:T(8,128)(2,1)} %get-tuple-element.38, ...), kind=kOutput, calls=%fused_computation.12 | convolution fusion | flops 22581870592 | bytes 59246592 | tf_op jit(solution)/shard_map/dot_general | solution.py:337
  527.3 6.7 fusion.8.u_ref
  534.0 399.5 %mlp_out.1 = bf16[1024,5376]{1,0:T(8,128)(2,1)} custom-call(bf16[512,5376]{1,0:T(8,128)(2,1)} %multiply_convert_fusion.hid_ref, bf16[512,5376]{1,0:T(8,128)(2,1)} %fusion.8.u_ref, bf16[5376,5376]{1,0:T(8,128)(2,1)} %w1_ref.1, bf16[5376,5376]{1,0:T(8,128)(2,1)} %w3_ref.1, bf16[5376,5376]{1,0:T(8,128)(2,1)} %w2_ref.1, bf16[512,5376]{1,0:T(8,128)(2,1)} %copy-done.3, ...), custom_call_target="tpu_custom_call" | custom-call | flops 118380036096 | bytes 206438400 | tf_op jit(solution)/shard_map/mlp_out/pallas_call | solution.py:265
  933.5 9.5 %copy.30 = bf16[1024,5376]{1,0:T(8,128)(2,1)} copy(bf16[1024,5376]{1,0:T(8,128)(2,1)} %mlp_out.1) | data formatting | bytes 22020096
  (26 shorter events, 0.1 us)
Async XLA Ops:
  7.2 10.0 %copy-start.11 = (f32[5376]{0:T(1024)S(1)}, f32[5376]{0:T(1024)}, u32[]{:S(2)}) copy-start(f32[5376]{0:T(1024)} %param.13) | copy-start | bytes 64516
  7.2 358.0 %all-gather.2.cloned.1.call-start = ((), (), s32[]{:S(2)}) async-start(), calls=%async_computation.2 | async-start | bytes 45416448 | tf_op jit(solution)/shard_map/all_gather | solution.py:314
  9.8 7.3 copy-start.2
  77.4 4.7 copy-start
  77.4 4.7 copy-start.1
  82.1 1.2 copy-start.6
  239.7 59.8 %collective-permute-start.3 = (bf16[512,1024]{0,1:T(8,128)(2,1)S(1)}, bf16[512,1024]{0,1:T(8,128)(2,1)S(1)}, u32[]{:S(2)}, u32[]{:S(2)}) collective-permute-start(bf16[512,1024]{0,1:T(8,128)(2,1)S(1)} %bitcast.38), channel_id=1, source_target_pairs={{4,0},{8,4},{12,8},{5,1},{9,5},{13,9},{6,2},{10,6},{14,10},{7,3},{... | collective-permute-start | bytes 3145736 | tf_op jit(solution)/shard_map/ppermute | solution.py:101
  241.0 59.8 %collective-permute-start = (bf16[512,1024]{0,1:T(8,128)(2,1)S(1)}, bf16[512,1024]{0,1:T(8,128)(2,1)S(1)}, u32[]{:S(2)}, u32[]{:S(2)}) collective-permute-start(bf16[512,1024]{0,1:T(8,128)(2,1)S(1)} %bitcast.39), channel_id=1, source_target_pairs={{0,4},{4,8},{8,12},{1,5},{5,9},{9,13},{2,6},{6,10},{10,14},{3,7},{... | collective-permute-start | bytes 3145736 | tf_op jit(solution)/shard_map/ppermute | solution.py:100
  299.5 1.3 copy-start.7
  299.5 27.1 %collective-permute-start.4 = (bf16[512,1024]{0,1:T(8,128)(2,1)S(1)}, bf16[512,1024]{0,1:T(8,128)(2,1)}, u32[]{:S(2)}, u32[]{:S(2)}) collective-permute-start(bf16[512,1024]{0,1:T(8,128)(2,1)S(1)} %collective-permute-done.3), channel_id=1, source_target_pairs={{4,0},{8,4},{5,1},{9,5},{6,2},{10,6},{7,3},{11,7},{20,16},{24,20},... | collective-permute-start | bytes 3145736 | tf_op jit(solution)/shard_map/ppermute | solution.py:101
  300.8 25.8 %copy-start.8 = (bf16[512,1024]{0,1:T(8,128)(2,1)}, bf16[512,1024]{0,1:T(8,128)(2,1)S(1)}, u32[]{:S(2)}) copy-start(bf16[512,1024]{0,1:T(8,128)(2,1)S(1)} %collective-permute-done) | copy-start | bytes 3145732
  300.8 27.1 %collective-permute-start.1 = (bf16[512,1024]{0,1:T(8,128)(2,1)S(1)}, bf16[512,1024]{0,1:T(8,128)(2,1)}, u32[]{:S(2)}, u32[]{:S(2)}) collective-permute-start(bf16[512,1024]{0,1:T(8,128)(2,1)S(1)} %collective-permute-done), channel_id=1, source_target_pairs={{4,8},{8,12},{5,9},{9,13},{6,10},{10,14},{7,11},{11,15},{20,24},{2... | collective-permute-start | bytes 3145736 | tf_op jit(solution)/shard_map/ppermute | solution.py:100
  326.6 26.5 %collective-permute-start.5 = (bf16[512,1024]{0,1:T(8,128)(2,1)}, bf16[512,1024]{0,1:T(8,128)(2,1)}, u32[]{:S(2)}, u32[]{:S(2)}) collective-permute-start(bf16[512,1024]{0,1:T(8,128)(2,1)} %collective-permute-done.4), channel_id=1, source_target_pairs={{4,0},{5,1},{6,2},{7,3},{20,16},{21,17},{22,18},{23,19}} | collective-permute-start | bytes 3145736 | tf_op jit(solution)/shard_map/ppermute | solution.py:101
  327.9 25.2 %collective-permute-start.2 = (bf16[512,1024]{0,1:T(8,128)(2,1)}, bf16[512,1024]{0,1:T(8,128)(2,1)}, u32[]{:S(2)}, u32[]{:S(2)}) collective-permute-start(bf16[512,1024]{0,1:T(8,128)(2,1)} %collective-permute-done.1), channel_id=1, source_target_pairs={{8,12},{9,13},{10,14},{11,15},{24,28},{25,29},{26,30},{27,31}} | collective-permute-start | bytes 3145736 | tf_op jit(solution)/shard_map/ppermute | solution.py:100
  333.1 26.5 %copy-start.4 = (bf16[512,4,256]{0,2,1:T(8,128)(2,1)}, bf16[512,4,256]{0,2,1:T(8,128)(2,1)S(1)}, u32[]{:S(2)}) copy-start(bf16[512,4,256]{0,2,1:T(8,128)(2,1)S(1)} %copy.24) | copy-start | bytes 3145732
  358.2 41.1 %copy-start.9 = (f32[5376]{0:T(1024)S(1)}, f32[5376]{0:T(1024)}, u32[]{:S(2)}) copy-start(f32[5376]{0:T(1024)} %param.14) | copy-start | bytes 64516
  358.2 45.4 %collective-permute-start.7 = (bf16[512,1024]{0,1:T(8,128)(2,1)S(1)}, bf16[512,1024]{0,1:T(8,128)(2,1)}, u32[]{:S(2)}, u32[]{:S(2)}) collective-permute-start(bf16[512,1024]{0,1:T(8,128)(2,1)S(1)} %bitcast.35), channel_id=1, source_target_pairs={{4,0},{8,4},{12,8},{5,1},{9,5},{13,9},{6,2},{10,6},{14,10},{7,3},{... | collective-permute-start | bytes 3145736 | tf_op jit(solution)/shard_map/ppermute | solution.py:101
  359.7 44.0 %collective-permute-start.6 = (bf16[512,1024]{0,1:T(8,128)(2,1)S(1)}, bf16[512,1024]{0,1:T(8,128)(2,1)}, u32[]{:S(2)}, u32[]{:S(2)}) collective-permute-start(bf16[512,1024]{0,1:T(8,128)(2,1)S(1)} %bitcast.36), channel_id=1, source_target_pairs={{0,4},{4,8},{8,12},{1,5},{5,9},{9,13},{2,6},{6,10},{10,14},{3,7},{... | collective-permute-start | bytes 3145736 | tf_op jit(solution)/shard_map/ppermute | solution.py:100
  397.0 2.4 copy-start.3
  403.7 42.7 %collective-permute-start.8 = (bf16[512,1024]{0,1:T(8,128)(2,1)}, bf16[512,1024]{0,1:T(8,128)(2,1)S(1)}, u32[]{:S(2)}, u32[]{:S(2)}) collective-permute-start(bf16[512,1024]{0,1:T(8,128)(2,1)} %collective-permute-done.6), channel_id=1, source_target_pairs={{4,8},{8,12},{5,9},{9,13},{6,10},{10,14},{7,11},{11,15},{20,24},{2... | collective-permute-start | bytes 3145736 | tf_op jit(solution)/shard_map/ppermute | solution.py:100
  404.4 41.9 %collective-permute-start.9 = (bf16[512,1024]{0,1:T(8,128)(2,1)}, bf16[512,1024]{0,1:T(8,128)(2,1)S(1)}, u32[]{:S(2)}, u32[]{:S(2)}) collective-permute-start(bf16[512,1024]{0,1:T(8,128)(2,1)} %collective-permute-done.7), channel_id=1, source_target_pairs={{4,0},{8,4},{5,1},{9,5},{6,2},{10,6},{7,3},{11,7},{20,16},{24,20},... | collective-permute-start | bytes 3145736 | tf_op jit(solution)/shard_map/ppermute | solution.py:101
  446.3 45.0 %copy-start.5 = (bf16[512,4,256]{0,2,1:T(8,128)(2,1)S(1)}, bf16[512,4,256]{0,2,1:T(8,128)(2,1)}, u32[]{:S(2)}) copy-start(bf16[512,4,256]{0,2,1:T(8,128)(2,1)} %copy-done.4) | copy-start | bytes 3145732
  446.4 44.9 %collective-permute-start.10 = (bf16[512,1024]{0,1:T(8,128)(2,1)S(1)}, bf16[512,1024]{0,1:T(8,128)(2,1)S(1)}, u32[]{:S(2)}, u32[]{:S(2)}) collective-permute-start(bf16[512,1024]{0,1:T(8,128)(2,1)S(1)} %collective-permute-done.8), channel_id=1, source_target_pairs={{8,12},{9,13},{10,14},{11,15},{24,28},{25,29},{26,30},{27,31}} | collective-permute-start | bytes 3145736 | tf_op jit(solution)/shard_map/ppermute | solution.py:100
  447.2 44.1 %collective-permute-start.11 = (bf16[512,1024]{0,1:T(8,128)(2,1)S(1)}, bf16[512,1024]{0,1:T(8,128)(2,1)S(1)}, u32[]{:S(2)}, u32[]{:S(2)}) collective-permute-start(bf16[512,1024]{0,1:T(8,128)(2,1)S(1)} %collective-permute-done.9), channel_id=1, source_target_pairs={{4,0},{5,1},{6,2},{7,3},{20,16},{21,17},{22,18},{23,19}} | collective-permute-start | bytes 3145736 | tf_op jit(solution)/shard_map/ppermute | solution.py:101
  494.3 32.9 %copy-start.10 = (f32[5376]{0:T(1024)S(1)}, f32[5376]{0:T(1024)}, u32[]{:S(2)}) copy-start(f32[5376]{0:T(1024)} %param.14) | copy-start | bytes 64516
Sparse Core Ops, SparseCore 0:
  10.9 286.5 all-gather.1
where the time goes:
time: 958 us; the launch traced here: 950 us
  Pallas kernels  447 us (47%)
  matrix products  188 us (20%)
  blocking collectives  105 us (11%)
  waiting for transfers between devices  97.7 us (10%)
  local copies, waits for them, and re-layouts  39.1 us (4%)
  other arithmetic  34.7 us (4%)
  starting transfers between devices  23.1 us (2%)
  between operations  14.9 us (2%)
    pallas_call x1, Pallas kernels, _mlp_out(): pl.pallas_call(functools.partial(_mlp_kernel, nc=nc, nt=nt), grid=(nt + 6...  399 us
    ppermute x6, waiting for transfers between devices, _hop(): dn = lax.ppermute(dn, 'tp', [(i, i - 1) for i in range(1, 5 - k)])  97.7 us
    dot_general x2, matrix products, mix(): o = jnp.dot(a, wo_all, preferred_element_type=jnp.float32)  64.7 us
    all_to_all x1, blocking collectives, local(): buf = lax.all_to_all(buf.transpose(1, 2, 0, 3), 'sp', 0, 0, tiled=True)  58.8 us
    pallas_call x1, Pallas kernels, _attention(): pl.pallas_call(functools.partial(_attn_kernel, heads=heads, per_src=m //...  47.9 us
    all_to_all x1, blocking collectives, local(): att = lax.all_to_all(att, 'sp', 0, 0, tiled=True)  46.6 us
    dot_general x1, matrix products, local(): h3 = jnp.dot(u0, w3, preferred_element_type=jnp.float32)  42.8 us
    dot_general x1, matrix products, local(): h1 = jnp.dot(u0, w1, preferred_element_type=jnp.float32)  40.6 us
  transfers between devices with their start and end apart: 13, of which 3 were waited for; matrix products, arithmetic and copies ran while one was open for 22% of the time, Pallas kernels for 5%

commit v1 on v0

--- a/solution.py
+++ b/solution.py
@@ -41,8 +41,8 @@
     return jnp.concatenate([t1 * c - t2 * s, t2 * c + t1 * s], axis=-1)
 
 
-def _attn_kernel(q_ref, k_ref, v_ref, o_ref, *, heads, per_src):
-    i = pl.program_id(0)
+def _attn_kernel(q_ref, k_ref, v_ref, o_ref, *, heads, per_src, c):
+    i = pl.program_id(0) * per_src + c
     scale = HEAD_DIM ** -0.5
     q = q_ref[0].reshape(heads * QB, HEAD_DIM)
     rows = heads * QB
@@ -76,21 +76,21 @@
         o_ref[0, :, h * HEAD_DIM:(h + 1) * HEAD_DIM] = o[h * QB:(h + 1) * QB]
 
 
-def _attention(buf, heads):
+def _attention(buf, heads, c):
     sp, _, m, dh = buf.shape
     per = m // QB
     n = sp * m
     return pl.pallas_call(
-        functools.partial(_attn_kernel, heads=heads, per_src=m // KB),
-        grid=(n // QB,),
+        functools.partial(_attn_kernel, heads=heads, per_src=per, c=c),
+        grid=(sp,),
         in_specs=[
-            pl.BlockSpec((1, heads, QB, dh), lambda i: (i // per, 0, i % per, 0)),
+            pl.BlockSpec((1, heads, QB, dh), lambda i: (i, 0, c, 0)),
             pl.BlockSpec((sp, 1, m, dh), lambda i: (0, heads, 0, 0)),
             pl.BlockSpec((sp, 1, m, dh), lambda i: (0, heads + 1, 0, 0)),
         ],
-        out_specs=pl.BlockSpec((1, QB, heads * dh), lambda i: (i // per, i % per, 0)),
-        out_shape=jax.ShapeDtypeStruct((sp, m, heads * dh), jnp.bfloat16),
-        cost_estimate=pl.CostEstimate(flops=4 * heads * n * n * dh, bytes_accessed=8 * n * dh * 2, transcendentals=heads * n * n // 2),
+        out_specs=pl.BlockSpec((1, QB, heads * dh), lambda i: (i, 0, 0)),
+        out_shape=jax.ShapeDtypeStruct((sp, QB, heads * dh), jnp.bfloat16),
+        cost_estimate=pl.CostEstimate(flops=heads * n * n * dh, bytes_accessed=8 * n * dh * 2, transcendentals=heads * n * n // 4),
         compiler_params=pltpu.CompilerParams(vmem_limit_bytes=48 * 1024 * 1024),
         name="attn",
     )(buf, buf, buf)
@@ -322,13 +322,17 @@
         buf = lax.all_to_all(buf.transpose(1, 2, 0, 3), "sp", 0, 0, tiled=True)
         ka = buf[:, qh].reshape(n, 1, HEAD_DIM)
         va = buf[:, qh + 1].reshape(n, 1, HEAD_DIM)
-        att = _attention(buf, qh)
-        att = lax.all_to_all(att, "sp", 0, 0, tiled=True)
-        att = att.transpose(1, 0, 2).reshape(m, ht * HEAD_DIM)
         mc = m // 2
-        a0, a1 = att[:mc], att[mc:]
-        hops = [(a0, a0)]
-        for k in range(1, 4):
+
+        def rows(b, c):
+            a = lax.all_to_all(_attention(b, qh, c), "sp", 0, 0, tiled=True)
+            return a.transpose(1, 0, 2).reshape(mc, ht * HEAD_DIM)
+
+        a0, buf = lax.optimization_barrier((rows(buf, 0), buf))
+        hops = [(a0, a0), _hop(a0, a0, 1)]
+        a1 = rows(buf, 1)
+        a1, hops[1] = lax.optimization_barrier((a1, hops[1]))
+        for k in range(2, 4):
             hops.append(_hop(*hops[-1], k))
         first = _side_by_side(a0, *zip(*hops[1:]), t)
         first, a1 = lax.optimization_barrier((first, a1))

time: 958 us -> 925 us (0.966)
  waiting for transfers between devices: 97.7 us -> 69.2 us
    ppermute x6, waiting for transfers between devices: 97.7 us -> 69.1 us  [_hop(): dn = lax.ppermute(dn, 'tp', [(i, i - 1) for i in range(1, 5 - k)])]
    unnamed x29 -> x31, local copies, waits for them, and re-layouts: 23.9 us -> 26.1 us
    pallas_call x1 -> x2, Pallas kernels: 47.9 us -> 46.4 us  [_attention(): pl.pallas_call(functools.partial(_attn_kernel, heads=heads, per_src=per,...]
    all_to_all x1 -> x2, blocking collectives: 46.6 us -> 45.4 us  [rows(): a = lax.all_to_all(_attention(b, qh, c), 'sp', 0, 0, tiled=True)]
  transfers between devices with their start and end apart: 13 -> 13, of which waited for: 3 -> 2; matrix products, arithmetic and copies ran while one was open for 22% -> 22% of each run, Pallas kernels for 5% -> 5%
where the time goes in v1:
time: 925 us; the launch traced here: 918 us
  Pallas kernels  444 us (48%)
  matrix products  187 us (20%)
  blocking collectives  104 us (11%)
  waiting for transfers between devices  69.2 us (7%)
  local copies, waits for them, and re-layouts  41.1 us (4%)
  other arithmetic  34.5 us (4%)
  starting transfers between devices  23.6 us (3%)
  between operations  14.9 us (2%)
    pallas_call x1, Pallas kernels, _mlp_out(): pl.pallas_call(functools.partial(_mlp_kernel, nc=nc, nt=nt), grid=(nt + 6...  397 us
    ppermute x6, waiting for transfers between devices, _hop(): dn = lax.ppermute(dn, 'tp', [(i, i - 1) for i in range(1, 5 - k)])  69.1 us
    dot_general x2, matrix products, mix(): o = jnp.dot(a, wo_all, preferred_element_type=jnp.float32)  64.5 us
    all_to_all x1, blocking collectives, local(): buf = lax.all_to_all(buf.transpose(1, 2, 0, 3), 'sp', 0, 0, tiled=True)  58.5 us
    pallas_call x2, Pallas kernels, _attention(): pl.pallas_call(functools.partial(_attn_kernel, heads=heads, per_src=per,...  46.4 us
    all_to_all x2, blocking collectives, rows(): a = lax.all_to_all(_attention(b, qh, c), 'sp', 0, 0, tiled=True)  45.4 us
    dot_general x1, matrix products, local(): h3 = jnp.dot(u0, w3, preferred_element_type=jnp.float32)  42.5 us
    dot_general x1, matrix products, local(): h1 = jnp.dot(u0, w1, preferred_element_type=jnp.float32)  40.4 us
  transfers between devices with their start and end apart: 13, of which 2 were waited for; matrix products, arithmetic and copies ran while one was open for 22% of the time, Pallas kernels for 5%

profile of v1, /device:TPU:0, one launch (start us, length us, event | category | flops | bytes accessed | tf_op | source)
XLA Modules:
  0.0 918.0 jit_solution(9059428888219543269)
XLA Ops:
  7.2 0.0 all-gather.2.cloned.1.call-start
  7.2 2.5 constant_dynamic-slice_fusion
  9.8 0.0 all-gather.2.cloned.1.call-update
  9.8 0.0 copy-start.4
  9.8 0.8 convert_element_type.52
  10.7 6.5 fusion
  17.1 9.8 %convolution_convert_fusion = bf16[1024,512]{0,1:T(8,128)(2,1)} fusion(bf16[5376,512]{1,0:T(8,128)(2,1)} %param.17, bf16[1024,5376]{1,0:T(8,128)(2,1)S(1)} %copy-done.4, f32[5376]{0:T(1024)S(1)} %copy-done.12, f32[1024]{0:T(1024)S(1)} %add_rsqrt_fusion), kind=kOutput, calls=%fused_computation.31 | convolution fusion | flops 5659688960 | bytes 17589248 | tf_op jit(solution)/shard_map/dot_general | solution.py:320
  26.9 2.4 copy.22
  29.4 10.8 %fusion.20 = f32[1024,512]{0,1:T(8,128)S(1)} fusion(bf16[5376,512]{1,0:T(8,128)(2,1)} %param.16, bf16[1024,5376]{1,0:T(8,128)(2,1)} %param.11, f32[5376]{0:T(1024)S(1)} %copy-done.12, f32[1024]{0:T(1024)S(1)} %add_rsqrt_fusion), kind=kOutput, calls=%fused_computation.50 | convolution fusion | flops 5659164672 | bytes 18637824 | tf_op jit(solution)/shard_map/dot_general | solution.py:319
  40.2 1.2 fusion.26
  41.3 1.8 copy.28
  43.2 1.9 copy.27
  45.1 19.4 %fusion.22 = f32[1024,1024]{0,1:T(8,128)} fusion(bf16[5376,1024]{1,0:T(8,128)(2,1)} %param.15, bf16[1024,5376]{1,0:T(8,128)(2,1)} %param.11, f32[5376]{0:T(1024)S(1)} %copy-done.12, f32[1024]{0:T(1024)S(1)} %add_rsqrt_fusion), kind=kOutput, calls=%fused_computation.51 | convolution fusion | flops 11296309248 | bytes 26240000 | tf_op jit(solution)/shard_map/dot_general | solution.py:318
  64.5 4.8 fusion.25
  69.3 3.9 copy.26
  73.2 4.3 copy.25
  77.4 0.0 copy-start.2
  77.5 1.9 multiply_cosine_fusion
  79.4 2.7 fusion.16
  82.1 0.0 copy-start.8
  82.1 1.2 subtract_convert_fusion
  83.3 0.0 copy-done.8
  83.3 2.4 maximum_bitcast_fusion
  85.7 58.5 %all_to_all.15.q_ref.k_ref.v_ref = bf16[4,4,1024,128]{3,2,1,0:T(8,128)(2,1)S(1)} all-to-all(bf16[4,4,1024,128]{3,2,1,0:T(8,128)(2,1)S(1)} %maximum_bitcast_fusion), channel_id=1, replica_groups=mesh['rep'=2,'tp'=4,'sp'=4] {'sp'}, dimensions={0} | all-to-all | bytes 8388608 | tf_op jit(solution)/shard_map/all_to_all | solution.py:322
  144.2 20.6 %attn.2 = bf16[4,512,256]{2,1,0:T(8,128)(2,1)S(1)} custom-call(bf16[4,4,1024,128]{3,2,1,0:T(8,128)(2,1)S(1)} %all_to_all.15.q_ref.k_ref.v_ref, bf16[4,4,1024,128]{3,2,1,0:T(8,128)(2,1)S(1)} %all_to_all.15.q_ref.k_ref.v_ref, bf16[4,4,1024,128]{3,2,1,0:T(8,128)(2,1)S(1)} %all_to_all.15.q_ref.k_ref.v_ref), custom_call_target="tpu_custom_call" | custom-call | flops 4294967296 | bytes 8388608 | tf_op jit(solution)/shard_map/attn/pallas_call | solution.py:83
  164.9 28.5 %all_to_all.16 = bf16[4,512,256]{2,1,0:T(8,128)(2,1)S(1)} all-to-all(bf16[4,512,256]{2,1,0:T(8,128)(2,1)S(1)} %attn.2), channel_id=1, replica_groups=mesh['rep'=2,'tp'=4,'sp'=4] {'sp'}, dimensions={0} | all-to-all | bytes 2097152 | tf_op jit(solution)/shard_map/all_to_all | solution.py:328
  193.4 0.5 copy.23
  193.9 1.3 collective-permute-start.1
  195.2 5.5 collective-permute-start
  200.7 2.2 copy-done.1
  202.9 25.8 %attn.3 = bf16[4,512,256]{2,1,0:T(8,128)(2,1)S(1)} custom-call(bf16[4,4,1024,128]{3,2,1,0:T(8,128)(2,1)S(1)} %copy-done.1, bf16[4,4,1024,128]{3,2,1,0:T(8,128)(2,1)S(1)} %copy-done.1, bf16[4,4,1024,128]{3,2,1,0:T(8,128)(2,1)S(1)} %copy-done.1), custom_call_target="tpu_custom_call" | custom-call | flops 4294967296 | bytes 8388608 | tf_op jit(solution)/shard_map/attn/pallas_call | solution.py:83
  228.8 16.9 %all_to_all.17 = bf16[4,512,256]{2,1,0:T(8,128)(2,1)S(1)} all-to-all(bf16[4,512,256]{2,1,0:T(8,128)(2,1)S(1)} %attn.3), channel_id=1, replica_groups=mesh['rep'=2,'tp'=4,'sp'=4] {'sp'}, dimensions={0} | all-to-all | bytes 2097152 | tf_op jit(solution)/shard_map/all_to_all | solution.py:328
  245.6 0.5 copy.24
  246.2 0.0 collective-permute-done.1
  246.2 0.0 collective-permute-done
  246.2 0.7 collective-permute-start.2
  246.9 1.3 collective-permute-start.4
  248.2 0.0 collective-permute-done.2
  248.2 1.7 collective-permute-start.3
  249.9 46.2 %collective-permute-done.4 = bf16[512,1024]{0,1:T(8,128)(2,1)} collective-permute-done((bf16[512,1024]{0,1:T(8,128)(2,1)}, bf16[512,1024]{0,1:T(8,128)(2,1)}, u32[]{:S(2)}, u32[]{:S(2)}) %collective-permute-start.4) | collective-permute-done | bytes 1048608 | tf_op jit(solution)/shard_map/ppermute | solution.py:101
  296.2 1.5 collective-permute-start.5
  297.6 3.0 fusion.24
  300.7 0.0 collective-permute-done.3
  300.7 22.9 %collective-permute-done.5 = bf16[512,1024]{0,1:T(8,128)(2,1)} collective-permute-done((bf16[512,1024]{0,1:T(8,128)(2,1)}, bf16[512,1024]{0,1:T(8,128)(2,1)}, u32[]{:S(2)}, u32[]{:S(2)}) %collective-permute-start.5) | collective-permute-done | bytes 1048608 | tf_op jit(solution)/shard_map/ppermute | solution.py:101
  323.5 2.7 select_select_fusion.7
  326.3 2.2 pad_maximum_fusion
  328.4 1.4 collective-permute-start.7
  329.9 5.5 collective-permute-start.6
  335.4 31.6 %fusion.3 = (f32[512]{0:T(512)S(1)}, bf16[512,5376]{1,0:T(8,128)(2,1)S(1)}) fusion(bf16[512,4096]{0,1:T(8,128)(2,1)} %pad_maximum_fusion, bf16[4096,5376]{1,0:T(8,128)(2,1)} %all-gather.2.cloned.1.call-done, bf16[1024,5376]{1,0:T(8,128)(2,1)} %param.11), kind=kOutput, calls=%fused_computation.9 | convolution fusion | flops 22565093376 | bytes 59246592 | tf_op jit(solution)/shard_map/dot_general | solution.py:341
  367.0 2.3 copy-done.5
  369.4 4.3 fusion.5
  373.7 0.0 collective-permute-done.7
  373.7 0.7 collective-permute-start.8
  374.4 1.5 collective-permute-start.9
  376.0 40.4 %fusion.27 = f32[512,5376]{1,0:T(8,128)} fusion(bf16[512,5376]{1,0:T(8,128)(2,1)} %fusion.5, bf16[5376,5376]{1,0:T(8,128)(2,1)} %w1_ref.1), kind=kOutput, calls=%fused_computation.55 | convolution fusion | flops 29595009024 | bytes 74317824 | tf_op jit(solution)/shard_map/dot_general | solution.py:349
  416.4 0.9 collective-permute-start.10
  417.3 1.5 collective-permute-start.11
  418.8 42.5 %multiply_convert_fusion.hid_ref = bf16[512,5376]{1,0:T(8,128)(2,1)} fusion(f32[512,5376]{1,0:T(8,128)} %fusion.27, bf16[512,5376]{1,0:T(8,128)(2,1)} %fusion.5, bf16[5376,5376]{1,0:T(8,128)(2,1)} %w3_ref.1), kind=kOutput, calls=%fused_computation.16 | convolution fusion | flops 29611524096 | bytes 79822848 | tf_op jit(solution)/shard_map/dot_general | solution.py:352
  461.3 0.0 collective-permute-done.10
  461.3 3.0 select_select_fusion.3
  464.4 32.9 %fusion.6 = (f32[512]{0:T(512)S(1)}, bf16[512,5376]{1,0:T(8,128)(2,1)}) fusion(bf16[4096,5376]{1,0:T(8,128)(2,1)} %all-gather.2.cloned.1.call-done, bf16[512,1024]{0,1:T(8,128)(2,1)} %get-tuple-element.50, bf16[512,1024]{0,1:T(8,128)(2,1)} %get-tuple-element.49, bf16[512,1024]{0,1:T(8,128)(2,1)} %get-tuple-element.48, ...), kind=kOutput, calls=%fused_computation.12 | convolution fusion | flops 22581870592 | bytes 59246592 | tf_op jit(solution)/shard_map/dot_general | solution.py:341
  497.3 6.7 fusion.8.u_ref
  504.0 397.1 %mlp_out.1 = bf16[1024,5376]{1,0:T(8,128)(2,1)} custom-call(bf16[512,5376]{1,0:T(8,128)(2,1)} %multiply_convert_fusion.hid_ref, bf16[512,5376]{1,0:T(8,128)(2,1)} %fusion.8.u_ref, bf16[5376,5376]{1,0:T(8,128)(2,1)} %w1_ref.1, bf16[5376,5376]{1,0:T(8,128)(2,1)} %w3_ref.1, bf16[5376,5376]{1,0:T(8,128)(2,1)} %w2_ref.1, bf16[512,5376]{1,0:T(8,128)(2,1)} %copy-done.5, ...), custom_call_target="tpu_custom_call" | custom-call | flops 118380036096 | bytes 206438400 | tf_op jit(solution)/shard_map/mlp_out/pallas_call | solution.py:265
  901.1 9.5 %copy.30 = bf16[1024,5376]{1,0:T(8,128)(2,1)} copy(bf16[1024,5376]{1,0:T(8,128)(2,1)} %mlp_out.1) | data formatting | bytes 22020096
  (29 shorter events, 0.1 us)
Async XLA Ops:
  7.2 10.0 %copy-start.12 = (f32[5376]{0:T(1024)S(1)}, f32[5376]{0:T(1024)}, u32[]{:S(2)}) copy-start(f32[5376]{0:T(1024)} %param.13) | copy-start | bytes 64516
  7.2 328.2 %all-gather.2.cloned.1.call-start = ((), (), s32[]{:S(2)}) async-start(), calls=%async_computation.3 | async-start | bytes 45416448 | tf_op jit(solution)/shard_map/all_gather | solution.py:314
  9.8 7.3 copy-start.4
  77.4 4.7 copy-start.2
  77.4 4.7 copy-start.3
  82.1 1.2 copy-start.8
  144.2 49.2 %copy-start = (bf16[4,4,1024,128]{3,2,1,0:T(8,128)(2,1)}, bf16[4,4,1024,128]{3,2,1,0:T(8,128)(2,1)S(1)}, u32[]{:S(2)}) copy-start(bf16[4,4,1024,128]{3,2,1,0:T(8,128)(2,1)S(1)} %all_to_all.15.q_ref.k_ref.v_ref) | copy-start | bytes 12582916
  193.9 52.2 %collective-permute-start.1 = (bf16[512,1024]{0,1:T(8,128)(2,1)S(1)}, bf16[512,1024]{0,1:T(8,128)(2,1)}, u32[]{:S(2)}, u32[]{:S(2)}) collective-permute-start(bf16[512,1024]{0,1:T(8,128)(2,1)S(1)} %bitcast.34), channel_id=1, source_target_pairs={{4,0},{8,4},{12,8},{5,1},{9,5},{13,9},{6,2},{10,6},{14,10},{7,3},{... | collective-permute-start | bytes 3145736 | tf_op jit(solution)/shard_map/ppermute | solution.py:101
  195.2 51.0 %collective-permute-start = (bf16[512,1024]{0,1:T(8,128)(2,1)S(1)}, bf16[512,1024]{0,1:T(8,128)(2,1)}, u32[]{:S(2)}, u32[]{:S(2)}) collective-permute-start(bf16[512,1024]{0,1:T(8,128)(2,1)S(1)} %bitcast.35), channel_id=1, source_target_pairs={{0,4},{4,8},{8,12},{1,5},{5,9},{9,13},{2,6},{6,10},{10,14},{3,7},{... | collective-permute-start | bytes 3145736 | tf_op jit(solution)/shard_map/ppermute | solution.py:100
  200.7 2.2 copy-start.1
  246.1 83.7 %copy-start.6 = (bf16[512,4,256]{0,2,1:T(8,128)(2,1)}, bf16[512,4,256]{0,2,1:T(8,128)(2,1)S(1)}, u32[]{:S(2)}) copy-start(bf16[512,4,256]{0,2,1:T(8,128)(2,1)S(1)} %copy.24) | copy-start | bytes 3145732
  246.2 2.0 collective-permute-start.2
  246.9 49.3 %collective-permute-start.4 = (bf16[512,1024]{0,1:T(8,128)(2,1)}, bf16[512,1024]{0,1:T(8,128)(2,1)}, u32[]{:S(2)}, u32[]{:S(2)}) collective-permute-start(bf16[512,1024]{0,1:T(8,128)(2,1)} %collective-permute-done.1), channel_id=1, source_target_pairs={{4,0},{8,4},{5,1},{9,5},{6,2},{10,6},{7,3},{11,7},{20,16},{24,20},... | collective-permute-start | bytes 3145736 | tf_op jit(solution)/shard_map/ppermute | solution.py:101
  248.2 52.4 %copy-start.9 = (bf16[512,1024]{0,1:T(8,128)(2,1)}, bf16[512,1024]{0,1:T(8,128)(2,1)S(1)}, u32[]{:S(2)}) copy-start(bf16[512,1024]{0,1:T(8,128)(2,1)S(1)} %collective-permute-done.2) | copy-start | bytes 3145732
  248.2 52.4 %collective-permute-start.3 = (bf16[512,1024]{0,1:T(8,128)(2,1)S(1)}, bf16[512,1024]{0,1:T(8,128)(2,1)}, u32[]{:S(2)}, u32[]{:S(2)}) collective-permute-start(bf16[512,1024]{0,1:T(8,128)(2,1)S(1)} %collective-permute-done.2), channel_id=1, source_target_pairs={{8,12},{9,13},{10,14},{11,15},{24,28},{25,29},{26,30},{27,31}} | collective-permute-start | bytes 3145736 | tf_op jit(solution)/shard_map/ppermute | solution.py:100
  296.2 27.4 %collective-permute-start.5 = (bf16[512,1024]{0,1:T(8,128)(2,1)}, bf16[512,1024]{0,1:T(8,128)(2,1)}, u32[]{:S(2)}, u32[]{:S(2)}) collective-permute-start(bf16[512,1024]{0,1:T(8,128)(2,1)} %collective-permute-done.4), channel_id=1, source_target_pairs={{4,0},{5,1},{6,2},{7,3},{20,16},{21,17},{22,18},{23,19}} | collective-permute-start | bytes 3145736 | tf_op jit(solution)/shard_map/ppermute | solution.py:101
  328.4 40.9 %copy-start.10 = (f32[5376]{0:T(1024)S(1)}, f32[5376]{0:T(1024)}, u32[]{:S(2)}) copy-start(f32[5376]{0:T(1024)} %param.14) | copy-start | bytes 64516
  328.4 45.3 %collective-permute-start.7 = (bf16[512,1024]{0,1:T(8,128)(2,1)S(1)}, bf16[512,1024]{0,1:T(8,128)(2,1)}, u32[]{:S(2)}, u32[]{:S(2)}) collective-permute-start(bf16[512,1024]{0,1:T(8,128)(2,1)S(1)} %bitcast.31), channel_id=1, source_target_pairs={{4,0},{8,4},{12,8},{5,1},{9,5},{13,9},{6,2},{10,6},{14,10},{7,3},{... | collective-permute-start | bytes 3145736 | tf_op jit(solution)/shard_map/ppermute | solution.py:101
  329.9 43.9 %collective-permute-start.6 = (bf16[512,1024]{0,1:T(8,128)(2,1)S(1)}, bf16[512,1024]{0,1:T(8,128)(2,1)}, u32[]{:S(2)}, u32[]{:S(2)}) collective-permute-start(bf16[512,1024]{0,1:T(8,128)(2,1)S(1)} %bitcast.32), channel_id=1, source_target_pairs={{0,4},{4,8},{8,12},{1,5},{5,9},{9,13},{2,6},{6,10},{10,14},{3,7},{... | collective-permute-start | bytes 3145736 | tf_op jit(solution)/shard_map/ppermute | solution.py:100
  367.0 2.4 copy-start.5
  373.7 42.7 %collective-permute-start.8 = (bf16[512,1024]{0,1:T(8,128)(2,1)}, bf16[512,1024]{0,1:T(8,128)(2,1)S(1)}, u32[]{:S(2)}, u32[]{:S(2)}) collective-permute-start(bf16[512,1024]{0,1:T(8,128)(2,1)} %collective-permute-done.6), channel_id=1, source_target_pairs={{4,8},{8,12},{5,9},{9,13},{6,10},{10,14},{7,11},{11,15},{20,24},{2... | collective-permute-start | bytes 3145736 | tf_op jit(solution)/shard_map/ppermute | solution.py:100
  374.4 41.9 %collective-permute-start.9 = (bf16[512,1024]{0,1:T(8,128)(2,1)}, bf16[512,1024]{0,1:T(8,128)(2,1)S(1)}, u32[]{:S(2)}, u32[]{:S(2)}) collective-permute-start(bf16[512,1024]{0,1:T(8,128)(2,1)} %collective-permute-done.7), channel_id=1, source_target_pairs={{4,0},{8,4},{5,1},{9,5},{6,2},{10,6},{7,3},{11,7},{20,16},{24,20},... | collective-permute-start | bytes 3145736 | tf_op jit(solution)/shard_map/ppermute | solution.py:101
  416.4 45.0 %copy-start.7 = (bf16[512,4,256]{0,2,1:T(8,128)(2,1)S(1)}, bf16[512,4,256]{0,2,1:T(8,128)(2,1)}, u32[]{:S(2)}) copy-start(bf16[512,4,256]{0,2,1:T(8,128)(2,1)} %copy-done.6) | copy-start | bytes 3145732
  416.4 44.9 %collective-permute-start.10 = (bf16[512,1024]{0,1:T(8,128)(2,1)S(1)}, bf16[512,1024]{0,1:T(8,128)(2,1)S(1)}, u32[]{:S(2)}, u32[]{:S(2)}) collective-permute-start(bf16[512,1024]{0,1:T(8,128)(2,1)S(1)} %collective-permute-done.8), channel_id=1, source_target_pairs={{8,12},{9,13},{10,14},{11,15},{24,28},{25,29},{26,30},{27,31}} | collective-permute-start | bytes 3145736 | tf_op jit(solution)/shard_map/ppermute | solution.py:100
  417.3 44.1 %collective-permute-start.11 = (bf16[512,1024]{0,1:T(8,128)(2,1)S(1)}, bf16[512,1024]{0,1:T(8,128)(2,1)S(1)}, u32[]{:S(2)}, u32[]{:S(2)}) collective-permute-start(bf16[512,1024]{0,1:T(8,128)(2,1)S(1)} %collective-permute-done.9), channel_id=1, source_target_pairs={{4,0},{5,1},{6,2},{7,3},{20,16},{21,17},{22,18},{23,19}} | collective-permute-start | bytes 3145736 | tf_op jit(solution)/shard_map/ppermute | solution.py:101
  464.4 32.9 %copy-start.11 = (f32[5376]{0:T(1024)S(1)}, f32[5376]{0:T(1024)}, u32[]{:S(2)}) copy-start(f32[5376]{0:T(1024)} %param.14) | copy-start | bytes 64516
Sparse Core Ops, SparseCore 0:
  10.9 277.0 all-gather.1
